TPU v7x, 32 devices: a whole 2x2x4 slice. The times are simulated.
32 devices in a mesh: gx: 4 (over z), gy: 8 (over y, x, core).
Axes of the slice: x: 2, y: 2, z: 4, core: 2. Of those that a mesh axis runs over, the one named last changes fastest.
Arguments:
- spectrum: float32 [2, 256, 16384], P(None, ('gx', 'gy')), may hold values from -6 to 6
- parameters: float32 [2], replicated, may hold values from -1.5 to 1.5
Outputs:
- advanced: float32 [2, 256, 16384], P(None, ('gx', 'gy'))
All inputs are finite; a program needn't handle non-finite values.
Results may differ from a plain program's by a relative error of at most 0.0003.
Values sent between devices are 32-bit elements; how exact they have to be, the bound alone decides.
A program may use at most 128 MiB of HBM per device.

v0:
```python
import math

import jax
import jax.numpy as jnp
from jax import lax
from jax.sharding import PartitionSpec as P

time_step = 0.1
spacing = 0.25
highest = lax.Precision.HIGHEST


def angle_tables(rows_idx, cols_idx, length, orient):
    product = rows_idx[:, None] * cols_idx[None, :] % length
    angles = product.astype(jnp.float32) * (2.0 * math.pi / length)
    return (jnp.cos(angles), orient * jnp.sin(angles))


def dft_tables(length, orient):
    counter = jnp.arange(length, dtype=jnp.int32)
    return angle_tables(counter, counter, length, orient)


def complex_section(formula, tables, parts):
    cosine, sine_part = tables
    former, latter = parts
    real_out = jnp.einsum(formula, cosine, former, precision=highest) - jnp.einsum(
        formula, sine_part, latter, precision=highest
    )
    imag_out = jnp.einsum(formula, cosine, latter, precision=highest) + jnp.einsum(
        formula, sine_part, former, precision=highest
    )
    return (real_out, imag_out)


def complex_times(factor, operand):
    return (
        factor[0] * operand[0] - factor[1] * operand[1],
        factor[0] * operand[1] + factor[1] * operand[0],
    )


def complex_over(operand, factor):
    denominator = factor[0] * factor[0] + factor[1] * factor[1]
    return (
        (operand[0] * factor[0] + operand[1] * factor[1]) / denominator,
        (operand[1] * factor[0] - operand[0] * factor[1]) / denominator,
    )


def radix_split(length):
    return (128, length // 128)


def dft_first(parts, orient):
    length, breadth = parts[0].shape
    radix_size, remain = radix_split(length)
    shaped = (
        parts[0].reshape(radix_size, remain, breadth),
        parts[1].reshape(radix_size, remain, breadth),
    )
    sectioned = complex_section("pq,qnk->pnk", dft_tables(radix_size, orient), shaped)
    turns = angle_tables(
        jnp.arange(radix_size, dtype=jnp.int32), jnp.arange(remain, dtype=jnp.int32), length, orient
    )
    turned = complex_times((turns[0][:, :, None], turns[1][:, :, None]), sectioned)
    finished = complex_section("rn,pnk->rpk", dft_tables(remain, orient), turned)
    return (finished[0].reshape(length, breadth), finished[1].reshape(length, breadth))


def dft_last(parts, orient):
    batch_rows, length = parts[0].shape
    radix_size, remain = radix_split(length)
    shaped = (
        parts[0].reshape(batch_rows, radix_size, remain),
        parts[1].reshape(batch_rows, radix_size, remain),
    )
    sectioned = complex_section("pq,bqn->bpn", dft_tables(radix_size, orient), shaped)
    turns = angle_tables(
        jnp.arange(radix_size, dtype=jnp.int32), jnp.arange(remain, dtype=jnp.int32), length, orient
    )
    turned = complex_times((turns[0][None], turns[1][None]), sectioned)
    finished = complex_section("rn,bpn->brp", dft_tables(remain, orient), turned)
    return (finished[0].reshape(batch_rows, length), finished[1].reshape(batch_rows, length))


def phi_values(zeta_real, zeta_imag):
    inside = zeta_real * zeta_real + zeta_imag * zeta_imag < 1.0
    guarded = (jnp.where(inside, 1.0, zeta_real), jnp.where(inside, 0.0, zeta_imag))
    growth = jnp.exp(guarded[0])
    phi_one = complex_over(
        (growth * jnp.cos(guarded[1]) - 1.0, growth * jnp.sin(guarded[1])), guarded
    )
    phi_two = complex_over((phi_one[0] - 1.0, phi_one[1]), guarded)
    phi_three = complex_over((phi_two[0] - 0.5, phi_two[1]), guarded)
    direct = [phi_one, phi_two, phi_three]
    result = []
    for phi_order in (1, 2, 3):
        running = (
            jnp.full_like(zeta_real, 1.0 / math.factorial(14 + phi_order)),
            jnp.zeros_like(zeta_real),
        )
        for degree in range(13, -1, -1):
            running = complex_times(running, (zeta_real, zeta_imag))
            running = (running[0] + 1.0 / math.factorial(degree + phi_order), running[1])
        chosen = direct[phi_order - 1]
        result.append(
            jnp.stack(
                [jnp.where(inside, running[0], chosen[0]), jnp.where(inside, running[1], chosen[1])]
            )
        )
    return result


def coefficients(mode_index, modes_total, dispersion):
    signed = jnp.where(mode_index < modes_total // 2, mode_index, mode_index - modes_total).astype(
        jnp.float32
    )
    wavenum = signed * (2.0 * math.pi / (modes_total * spacing))
    wave_square = wavenum * wavenum
    zeta_real = time_step * (1.0 - wave_square)
    zeta_imag = -(time_step * dispersion * wave_square)
    phi_one, phi_two, phi_three = phi_values(zeta_real, zeta_imag)
    half_weight = 0.5 * time_step * phi_values(0.5 * zeta_real, 0.5 * zeta_imag)[0]
    growth = jnp.exp(zeta_real)
    decay_full = jnp.stack([growth * jnp.cos(zeta_imag), growth * jnp.sin(zeta_imag)])
    halfway = jnp.exp(0.5 * zeta_real)
    decay_half = jnp.stack([halfway * jnp.cos(0.5 * zeta_imag), halfway * jnp.sin(0.5 * zeta_imag)])
    weight_one = time_step * (phi_one - 3.0 * phi_two + 4.0 * phi_three)
    weight_two = time_step * (phi_two - 2.0 * phi_three)
    weight_three = time_step * (4.0 * phi_three - phi_two)
    return (decay_full, decay_half, half_weight, weight_one, weight_two, weight_three)


def scaled_by(factor, operand):
    return jnp.stack(complex_times((factor[0], factor[1]), (operand[0], operand[1])))


def advance(current, nonlinear, weights):
    decay_full, decay_half, half_weight, weight_one, weight_two, weight_three = weights
    start_term = nonlinear(current)
    inner_one = scaled_by(decay_half, current) + scaled_by(half_weight, start_term)
    one_term = nonlinear(inner_one)
    inner_two = scaled_by(decay_half, current) + scaled_by(half_weight, one_term)
    two_term = nonlinear(inner_two)
    inner_three = scaled_by(decay_half, inner_one) + scaled_by(
        half_weight, 2.0 * two_term - start_term
    )
    three_term = nonlinear(inner_three)
    return (
        scaled_by(decay_full, current)
        + scaled_by(weight_one, start_term)
        + 2.0 * scaled_by(weight_two, one_term + two_term)
        + scaled_by(weight_three, three_term)
    )


def local(spectrum, parameters):
    devices = lax.axis_size(("gx", "gy"))
    device = lax.axis_index(("gx", "gy"))
    row_shard = spectrum.shape[1]
    columns = spectrum.shape[2]
    all_rows = row_shard * devices
    col_shard = columns // devices
    modes_total = all_rows * columns
    dispersion = parameters[0]
    cubic_twist = parameters[1]
    norm_scale = 1.0 / math.sqrt(modes_total)
    all_index = jnp.arange(all_rows, dtype=jnp.int32)
    all_cols = jnp.arange(columns, dtype=jnp.int32)
    row_index = device * row_shard + jnp.arange(row_shard, dtype=jnp.int32)
    col_index = device * col_shard + jnp.arange(col_shard, dtype=jnp.int32)
    inverse_turn = angle_tables(all_index, col_index, modes_total, 1.0)
    forward_turn = angle_tables(row_index, all_cols, modes_total, -1.0)

    def unfold_local(spectral):
        return jnp.stack(dft_first((spectral[0], spectral[1]), 1.0))

    def physics(received):
        physical = dft_last((received[0, 0], received[1, 0]), 1.0)
        phys_real = physical[0] * norm_scale
        phys_imag = physical[1] * norm_scale
        magnitude = phys_real * phys_real + phys_imag * phys_imag
        cubic_real = -magnitude * (phys_real - cubic_twist * phys_imag)
        cubic_imag = -magnitude * (phys_imag + cubic_twist * phys_real)
        return jnp.stack(dft_last((cubic_real, cubic_imag), -1.0))[:, None]

    def finish(received):
        spectral = dft_first((received[0, :, 0], received[1, :, 0]), -1.0)
        return jnp.stack([spectral[0] * norm_scale, spectral[1] * norm_scale])[:, :, None]

    def physical_pass(opened):
        turned = jnp.stack(complex_times(inverse_turn, (opened[0], opened[1])))
        physical = physics(
            lax.all_to_all(
                turned.reshape(2, devices, row_shard, col_shard),
                ("gx", "gy"),
                split_axis=1,
                concat_axis=3,
                tiled=True,
            )
        )
        turned_back = jnp.stack(complex_times(forward_turn, (physical[0, 0], physical[1, 0])))
        spectral = finish(
            lax.all_to_all(
                turned_back.reshape(2, row_shard, devices, col_shard),
                ("gx", "gy"),
                split_axis=2,
                concat_axis=1,
                tiled=True,
            )
        )
        return spectral.reshape(2, all_rows, col_shard)

    weights = coefficients(
        all_index[:, None] * columns + col_index[None, :], modes_total, dispersion
    )

    def nonlinear_columns(spectral):
        return physical_pass(unfold_local(spectral))

    entered = lax.all_to_all(
        spectrum.reshape(2, row_shard, devices, col_shard),
        ("gx", "gy"),
        split_axis=2,
        concat_axis=1,
        tiled=True,
    )
    current = entered.reshape(2, all_rows, col_shard)
    current = advance(current, nonlinear_columns, weights)
    leaving = lax.all_to_all(
        current.reshape(2, devices, row_shard, col_shard),
        ("gx", "gy"),
        split_axis=1,
        concat_axis=3,
        tiled=True,
    )
    return leaving.reshape(2, row_shard, columns)


def solution(mesh):
    return jax.shard_map(
        local,
        mesh=mesh,
        in_specs=(P(None, ("gx", "gy"), None), P()),
        out_specs=P(None, ("gx", "gy"), None),
        check_vma=False,
    )
```

profile of v0, /device:TPU:0, one launch (start us, length us, event | category | flops | bytes accessed | tf_op | source)
XLA Modules:
  0.0 585.4 jit_solution(17083416606268591465)
XLA Ops:
  0.0 2.3 copy.736
  2.3 7.3 %all-to-all-start = ((f32[2,8,32,512]{3,1,0,2:T(8,128)}), f32[2,8,32,512]{3,1,0,2:T(8,128)S(1)}, u32[]{:S(2)}, u32[]{:S(2)}) async-start(f32[2,8,32,512]{3,1,0,2:T(8,128)} %bitcast.562), calls=%async_computation | async-start | bytes 2097152 | tf_op jit(solution)/shard_map/all_to_all | solution.py:222
  9.7 26.1 %all-to-all-done = f32[2,8,32,512]{3,1,0,2:T(8,128)S(1)} async-done(((f32[2,8,32,512]{3,1,0,2:T(8,128)}), f32[2,8,32,512]{3,1,0,2:T(8,128)S(1)}, u32[]{:S(2)}, u32[]{:S(2)}) %all-to-all-start) | async-done | bytes 1048608 | tf_op jit(solution)/shard_map/all_to_all | solution.py:222
  40.3 2.1 fusion.270
  44.4 2.1 convolution_add_fusion.7
  46.6 2.3 convolution_subtract_fusion.7
  49.1 2.3 multiply_subtract_fusion.26
  52.5 3.6 all-to-all-start.1
  59.7 22.6 %all-to-all-done.1 = f32[2,32,8,512]{3,2,0,1:T(8,128)S(1)} async-done(((f32[2,32,8,512]{3,2,0,1:T(8,128)}), f32[2,32,8,512]{3,2,0,1:T(8,128)S(1)}, u32[]{:S(2)}, u32[]{:S(2)}) %all-to-all-start.1) | async-done | bytes 1048608 | tf_op jit(solution)/shard_map/all_to_all | solution.py:195
  107.5 2.4 multiply_subtract_fusion.23
  111.6 3.7 all-to-all-start.2
  115.3 14.8 %fusion.70 = (f32[1,256,512]{2,1,0:T(8,128)S(1)}, f32[1,256,512]{2,1,0:T(8,128)}, f32[1,256,512]{2,1,0:T(8,128)S(1)}, f32[1,256,512]{2,1,0:T(8,128)S(1)}, f32[1,...) fusion(f32[]{:T(128)} %bitcast, ...), kind=kLoop, calls=%fused_computation.177 | loop fusion | flops 61997056 | bytes 6294532 | tf_op jit(solution)/shard_map/sub | solution.py:38
  130.1 2.2 subtract_multiply_fusion
  132.3 9.2 %all-to-all-done.2 = f32[2,8,32,512]{3,1,0,2:T(8,128)} async-done(((f32[2,8,32,512]{3,1,0,2:T(8,128)}), f32[2,8,32,512]{3,1,0,2:T(8,128)}, u32[]{:S(2)}, u32[]{:S(2)}) %all-to-all-start.2) | async-done | bytes 1048608 | tf_op jit(solution)/shard_map/all_to_all | solution.py:205
  141.5 2.2 fusion.1104
  155.4 2.2 fusion.1
  157.7 2.6 fusion
  162.0 3.4 multiply_subtract_fusion.7
  171.7 2.1 fusion.258
  175.8 2.1 convolution_add_fusion.5
  178.1 2.3 convolution_subtract_fusion.5
  180.5 2.3 multiply_subtract_fusion.19
  183.0 29.6 %all_to_all.150 = f32[2,32,8,512]{3,2,0,1:T(8,128)S(1)} all-to-all(f32[2,32,8,512]{3,2,0,1:T(8,128)S(1)} %copy.435), channel_id=1, replica_groups=mesh['gx'=4,'gy'=8] {'gx','gy'}, dimensions={1} | all-to-all | bytes 2097152 | tf_op jit(solution)/shard_map/all_to_all | solution.py:195
  239.3 3.0 fusion.21
  245.6 2.4 multiply_subtract_fusion.16
  248.7 29.6 %all_to_all.151 = f32[2,8,32,512]{3,1,0,2:T(8,128)S(1)} all-to-all(f32[2,8,32,512]{3,1,0,2:T(8,128)S(1)} %copy.452), channel_id=1, replica_groups=mesh['gx'=4,'gy'=8] {'gx','gy'}, dimensions={2} | all-to-all | bytes 2097152 | tf_op jit(solution)/shard_map/all_to_all | solution.py:205
  289.6 2.2 fusion.3
  291.9 2.4 fusion.2
  305.3 2.1 fusion.250
  307.3 2.5 convolution_add_fusion.3
  310.0 2.1 convolution_subtract_fusion.3
  312.2 2.3 multiply_subtract_fusion.12
  314.7 29.6 %all_to_all.152 = f32[2,32,8,512]{3,2,0,1:T(8,128)S(1)} all-to-all(f32[2,32,8,512]{3,2,0,1:T(8,128)S(1)} %copy.473), channel_id=1, replica_groups=mesh['gx'=4,'gy'=8] {'gx','gy'}, dimensions={1} | all-to-all | bytes 2097152 | tf_op jit(solution)/shard_map/all_to_all | solution.py:195
  371.0 3.0 fusion.15
  377.3 2.4 multiply_subtract_fusion.9
  380.4 29.6 %all_to_all.153 = f32[2,8,32,512]{3,1,0,2:T(8,128)S(1)} all-to-all(f32[2,8,32,512]{3,1,0,2:T(8,128)S(1)} %copy.490), channel_id=1, replica_groups=mesh['gx'=4,'gy'=8] {'gx','gy'}, dimensions={2} | all-to-all | bytes 2097152 | tf_op jit(solution)/shard_map/all_to_all | solution.py:205
  421.3 2.2 fusion.5
  423.6 2.7 fusion.4
  440.6 2.3 convolution_add_fusion.1
  443.0 2.1 convolution_subtract_fusion.1
  445.2 5.8 multiply_subtract_fusion.4
  451.2 29.6 %all_to_all.154 = f32[2,32,8,512]{3,2,0,1:T(8,128)S(1)} all-to-all(f32[2,32,8,512]{3,2,0,1:T(8,128)S(1)} %copy.511), channel_id=1, replica_groups=mesh['gx'=4,'gy'=8] {'gx','gy'}, dimensions={1} | all-to-all | bytes 2097152 | tf_op jit(solution)/shard_map/all_to_all | solution.py:195
  504.1 2.4 multiply_subtract_fusion.1
  508.2 3.8 all-to-all-start.8
  513.2 24.8 %all-to-all-done.8 = f32[2,8,32,512]{3,1,0,2:T(8,128)S(1)} async-done(((f32[2,8,32,512]{3,1,0,2:T(8,128)}), f32[2,8,32,512]{3,1,0,2:T(8,128)S(1)}, u32[]{:S(2)}, u32[]{:S(2)}) %all-to-all-start.8) | async-done | bytes 1048608 | tf_op jit(solution)/shard_map/all_to_all | solution.py:205
  546.5 2.2 fusion.7
  548.8 2.4 fusion.6
  553.8 29.6 %all_to_all.155 = f32[2,32,8,512]{3,2,0,1:T(8,128)S(1)} all-to-all(f32[2,32,8,512]{3,2,0,1:T(8,128)S(1)} %copy.539), channel_id=1, replica_groups=mesh['gx'=4,'gy'=8] {'gx','gy'}, dimensions={1} | all-to-all | bytes 2097152 | tf_op jit(solution)/shard_map/all_to_all | solution.py:231
  (301 shorter events, 207.0 us)
Async XLA Ops:
  2.3 33.5 %all-to-all-start = ((f32[2,8,32,512]{3,1,0,2:T(8,128)}), f32[2,8,32,512]{3,1,0,2:T(8,128)S(1)}, u32[]{:S(2)}, u32[]{:S(2)}) async-start(f32[2,8,32,512]{3,1,0,2:T(8,128)} %bitcast.562), calls=%async_computation | async-start | bytes 2097152 | tf_op jit(solution)/shard_map/all_to_all | solution.py:222
  52.5 29.8 %all-to-all-start.1 = ((f32[2,32,8,512]{3,2,0,1:T(8,128)}), f32[2,32,8,512]{3,2,0,1:T(8,128)S(1)}, u32[]{:S(2)}, u32[]{:S(2)}) async-start(f32[2,32,8,512]{3,2,0,1:T(8,128)} %copy.395), calls=%async_computation.1 | async-start | bytes 2097152 | tf_op jit(solution)/shard_map/all_to_all | solution.py:195
  57.2 0.7 copy-start.37
  111.6 29.9 %all-to-all-start.2 = ((f32[2,8,32,512]{3,1,0,2:T(8,128)}), f32[2,8,32,512]{3,1,0,2:T(8,128)}, u32[]{:S(2)}, u32[]{:S(2)}) async-start(f32[2,8,32,512]{3,1,0,2:T(8,128)} %copy.414), calls=%async_computation.2 | async-start | bytes 2097152 | tf_op jit(solution)/shard_map/all_to_all | solution.py:205
  130.1 31.7 %copy-start.8 = (f32[1,256,512]{2,1,0:T(8,128)}, f32[1,256,512]{2,1,0:T(8,128)S(1)}, u32[]{:S(2)}) copy-start(f32[1,256,512]{2,1,0:T(8,128)S(1)} %get-tuple-element.40) | copy-start | bytes 1572868
  145.1 1.7 copy-start.12
  148.1 1.0 copy-start.23
  149.2 1.0 copy-start.13
  157.7 2.7 copy-start
  157.7 2.7 copy-start.16
  160.4 1.4 copy-start.2
  160.4 1.4 copy-start.10
  168.8 1.0 copy-start.28
  213.9 1.9 copy-start.31
  218.0 1.1 copy-start.21
  244.4 1.2 copy-start.19
  282.5 1.0 copy-start.24
  291.9 2.5 copy-start.4
  294.4 0.8 copy-start.6
  294.4 1.2 copy-start.9
  294.4 1.4 copy-start.11
  300.2 1.0 copy-start.25
  345.6 1.9 copy-start.32
  349.7 1.1 copy-start.22
  376.1 1.2 copy-start.20
  414.3 1.0 copy-start.26
  423.6 2.8 copy-start.5
  423.6 2.8 copy-start.7
  426.3 1.0 copy-start.1
  426.3 1.2 copy-start.3
  427.9 1.0 copy-start.33
  427.9 1.2 copy-start.34
  433.5 1.0 copy-start.27
  508.2 3.8 copy-start.15
  508.2 29.8 %all-to-all-start.8 = ((f32[2,8,32,512]{3,1,0,2:T(8,128)}), f32[2,8,32,512]{3,1,0,2:T(8,128)S(1)}, u32[]{:S(2)}, u32[]{:S(2)}) async-start(f32[2,8,32,512]{3,1,0,2:T(8,128)} %copy.528), calls=%async_computation.8 | async-start | bytes 2097152 | tf_op jit(solution)/shard_map/all_to_all | solution.py:205
  548.8 2.6 copy-start.14
  551.3 1.0 copy-start.17
  551.3 1.2 copy-start.18
  551.4 1.3 copy-start.29
  551.4 1.5 copy-start.30
  551.4 1.6 copy-start.35
  551.4 1.8 copy-start.36
where the time goes:
time: 596 us; the launch traced here: 585 us
  matrix products  186 us (31%)
  blocking collectives  178 us (30%)
  waiting for transfers between devices  82.8 us (14%)
  local copies, waits for them, and re-layouts  67.7 us (11%)
  other arithmetic  48.9 us (8%)
  starting transfers between devices  18.5 us (3%)
    all_to_all x3, blocking collectives, physical_pass(): lax.all_to_all(turned.reshape(2, devices, row_shard, col_shard), ('gx', '...  88.9 us
    all_to_all x2, blocking collectives, physical_pass(): lax.all_to_all(turned_back.reshape(2, row_shard, devices, col_shard), ('g...  59.3 us
    dot_general x32, matrix products, complex_section(): jnp.einsum(formula, sine_part, latter, precision=highest)  49.4 us
    dot_general x32, matrix products, complex_section(): jnp.einsum(formula, cosine, former, precision=highest)  47.2 us
    dot_general x32, matrix products, complex_section(): jnp.einsum(formula, sine_part, former, precision=highest)  45.5 us
    dot_general x32, matrix products, complex_section(): jnp.einsum(formula, cosine, latter, precision=highest)  44.4 us
    sub x13, other arithmetic, complex_times(): factor[0] * operand[0] - factor[1] * operand[1]  42.2 us
    all_to_all x2, waiting for transfers between devices, physical_pass(): lax.all_to_all(turned_back.reshape(2, row_shard, devices, col_shard), ('g...  34 us
  transfers between devices with their start and end apart: 4, of which 4 were waited for; matrix products, arithmetic and copies ran while one was open for 3% of the time, Pallas kernels for 0%

commit v1 on v0

v1 whole, which is shorter than its diff:
```python
import functools
import math

import jax
import jax.numpy as jnp
import numpy as np
from jax import lax
from jax.experimental import pallas as pl
from jax.experimental.pallas import tpu as pltpu
from jax.sharding import PartitionSpec as P

time_step = 0.1
spacing = 0.25
lanes = 128
sublanes = 8


def real_form(matrix):
    return np.block([[matrix.real, -matrix.imag], [matrix.imag, matrix.real]])


def halves(matrix):
    high = jnp.asarray(matrix, jnp.float32).astype(jnp.bfloat16)
    low = (jnp.asarray(matrix, jnp.float32) - high.astype(jnp.float32)).astype(jnp.bfloat16)
    return high, low


def unit_roots(left, right, length):
    product = (left[:, None].astype(np.int64) * right[None, :].astype(np.int64)) % length
    return np.exp(2j * np.pi * product / length)


def split(value):
    high = value.astype(jnp.bfloat16)
    return high, (value - high.astype(jnp.float32)).astype(jnp.bfloat16)


def dot(a, b):
    return jnp.dot(a, b, preferred_element_type=jnp.float32)


def dot3(left, right):
    return dot(left[0], right[0]) + dot(left[0], right[1]) + dot(left[1], right[0])


def times(a, b):
    return a[0] * b[0] - a[1] * b[1], a[0] * b[1] + a[1] * b[0]


def phi_values(w, orders):
    inside = w[0] * w[0] + w[1] * w[1] < 1.0
    g = (jnp.where(inside, 1.0, w[0]), jnp.where(inside, 0.0, w[1]))
    inverse = 1.0 / (g[0] * g[0] + g[1] * g[1])
    inv = (g[0] * inverse, -g[1] * inverse)
    growth = jnp.exp(g[0])
    direct = []
    last = (growth * jnp.cos(g[1]), growth * jnp.sin(g[1]))
    for k in range(orders):
        last = times((last[0] - 1.0 / math.factorial(k), last[1]), inv)
        direct.append(last)
    running = (
        jnp.full_like(w[0], 1.0 / math.factorial(14 + orders)),
        jnp.zeros_like(w[0]),
    )
    for degree in range(13, -1, -1):
        running = times(running, w)
        running = (running[0] + 1.0 / math.factorial(degree + orders), running[1])
    series = [running]
    for k in range(orders - 1, 0, -1):
        running = times(running, w)
        running = (running[0] + 1.0 / math.factorial(k), running[1])
        series.insert(0, running)
    return [
        (jnp.where(inside, s[0], d[0]), jnp.where(inside, s[1], d[1]))
        for s, d in zip(series, direct)
    ]


def weights_at(mode, modes_total, dispersion):
    signed = jnp.where(mode < modes_total // 2, mode, mode - modes_total).astype(jnp.float32)
    wavenum = signed * (2.0 * math.pi / (modes_total * spacing))
    square = wavenum * wavenum
    zeta = (time_step * (1.0 - square), -(time_step * dispersion * square))
    half = (0.5 * zeta[0], 0.5 * zeta[1])
    one, two, three = phi_values(zeta, 3)
    (half_one,) = phi_values(half, 1)
    grow = jnp.exp(half[0])
    e2 = (grow * jnp.cos(half[1]), grow * jnp.sin(half[1]))
    full = times(e2, e2)
    h = time_step
    q = tuple(0.5 * h * x for x in half_one)
    f1 = tuple(h * (a - 3.0 * b + 4.0 * c) for a, b, c in zip(one, two, three))
    f2 = tuple(2.0 * h * (b - 2.0 * c) for b, c in zip(two, three))
    f3 = tuple(h * (4.0 * c - b) for b, c in zip(two, three))
    return full, e2, q, f1, f2, f3


def kernel(
    axes, sizes,
    par_ref, spec_ref, m1h, m1l, m2h, m2l, n2h, n2l, m3h, m3l, n3h, n3l, t2_ref,
    out_ref,
    send, recv, wts, t1, pre, acc, astate, nl, xah, xal, xbh, xbl, pxh, pxl, send_sem, recv_sem,
):
    Z, G, D, K, R = sizes
    A = K * D
    cols = A * lanes
    span = K * lanes
    total = R * cols
    zi = lax.axis_index(axes[0])
    gi = lax.axis_index(axes[1])
    me = zi * G + gi
    mesh_type = pl.DeviceIdType.MESH
    beta = par_ref[1]

    chunks = 2 if K % 2 == 0 else 1
    part_k = K // chunks

    def peer_at(i):
        mask = D - i
        if D & (D - 1) == 0:
            peer, bit = 0, 1
            while bit < D:
                peer = peer + lax.rem(me // bit + mask // bit, 2) * bit
                bit *= 2
        else:
            peer = lax.rem(me + mask, D)
        return peer // G, lax.rem(peer, G)

    def copy(slot, chunk, i, landing):
        pz, pg = peer_at(i)
        peer = pz * G + pg
        at = me if landing is None else peer
        ks = pl.ds(chunk * part_k, part_k)
        return pltpu.make_async_remote_copy(
            src_ref=send.at[:, ks, peer],
            dst_ref=recv.at[slot, :, ks, at],
            send_sem=send_sem.at[chunk, peer],
            recv_sem=recv_sem.at[slot, chunk, at],
            device_id=(pz, pg),
            device_id_type=mesh_type,
        )

    def start(slot, chunk):
        def body(i, carry):
            copy(slot, chunk, i, None).start()
            return carry

        lax.fori_loop(1, D, body, 0)
        for k in range(chunk * part_k, (chunk + 1) * part_k):
            recv[slot, :, k, me] = send[:, k, me]

    def finish(slot, chunk):
        def body(i, carry):
            arriving = copy(slot, chunk, i, True)
            arriving.wait_recv()
            arriving.wait_send()
            return carry

        lax.fori_loop(1, D, body, 0)

    def loop(count, body):
        def wrapped(i, carry):
            body(i)
            return carry

        lax.fori_loop(0, count, wrapped, 0)

    barrier = pltpu.get_barrier_semaphore()

    def greet(i):
        pz, pg = peer_at(i + 1)
        pl.semaphore_signal(barrier, inc=1, device_id=(pz, pg), device_id_type=mesh_type)

    loop(D - 1, greet)

    def enter(d):
        for k in range(K):
            at = pl.multiple_of(d * span + k * lanes, lanes)
            send[:, k, d] = spec_ref[:, :, pl.ds(at, lanes)]

    loop(D, enter)
    pl.semaphore_wait(barrier, D - 1)
    for chunk in range(chunks):
        start(0, chunk)

    rows_w = 16
    norm = 1.0 / math.sqrt(total)

    def prepare(b):
        k = lax.rem(b, K)
        r0 = pl.multiple_of(b // K * rows_w, rows_w)
        row = r0 + lax.broadcasted_iota(jnp.int32, (rows_w, lanes), 0)
        lane = lax.broadcasted_iota(jnp.int32, (rows_w, lanes), 1)
        col = me * span + k * lanes + lane
        angle = (row * col).astype(jnp.float32) * (2.0 * math.pi / total)
        t1[0, k, pl.ds(r0, rows_w)] = norm * jnp.cos(angle)
        t1[1, k, pl.ds(r0, rows_w)] = norm * jnp.sin(angle)
        for n, w in enumerate(weights_at(row * cols + col, total, par_ref[0])):
            wts[n, 0, k, pl.ds(r0, rows_w)] = w[0]
            wts[n, 1, k, pl.ds(r0, rows_w)] = w[1]

    loop(R // rows_w * K, prepare)

    def flat(ref):
        return ref.reshape(2, K, R, lanes)

    rb = min(128, R)

    def pair(ref, k, at):
        return ref[0, k, pl.ds(at, rb)], ref[1, k, pl.ds(at, rb)]

    def put(ref, k, at, value):
        ref[0, k, pl.ds(at, rb)] = value[0]
        ref[1, k, pl.ds(at, rb)] = value[1]

    def put_split(high, low, k, at, value):
        for part in range(2):
            h, l = split(value[part])
            k0 = k % part_k * lanes
            high[pl.ds(part * R + at, rb), k0 : k0 + lanes] = h
            low[pl.ds(part * R + at, rb), k0 : k0 + lanes] = l

    def column_dot(high, low, at):
        right = (high[...], low[...])
        return tuple(
            dot3((m1h[pl.ds(part * R + at, rb), :], m1l[pl.ds(part * R + at, rb), :]), right)
            for part in range(2)
        )

    def lane_block(value, k):
        k0 = k % part_k * lanes
        return value[:, k0 : k0 + lanes]

    def blocks(chunk):
        return range(chunk * part_k, (chunk + 1) * part_k)

    def row_at(b):
        return pl.multiple_of(b * rb, rb)

    send_flat = flat(send)

    def launch(slot, chunk):
        def body(b):
            at = row_at(b)
            real, imag = column_dot(xbh, xbl, at)
            for k in blocks(chunk):
                turned = times((lane_block(real, k), lane_block(imag, k)), pair(t1, k, at))
                put(send_flat, k, at, turned)

        loop(R // rb, body)
        start(slot, chunk)

    def land(slot, chunk, use):
        arrived = flat(recv.at[slot])

        def turn(b):
            at = row_at(b)
            for k in blocks(chunk):
                x = pair(arrived, k, at)
                t = pair(t1, k, at)
                value = (x[0] * t[0] + x[1] * t[1], x[0] * t[1] - x[1] * t[0])
                put_split(xah, xal, k, at, value)

        loop(R // rb, turn)

        def body(b):
            at = row_at(b)
            real, imag = column_dot(xah, xal, at)
            for k in blocks(chunk):
                use(k, at, (lane_block(real, k), -lane_block(imag, k)))

        loop(R // rb, body)

    group = 4
    lines_out = send.reshape(2 * A * sublanes, lanes)

    def physics(slot):
        lines_in = recv.at[slot].reshape(2 * A * sublanes, lanes)
        tr, ti = t2_ref[0], t2_ref[1]
        for base in range(0, sublanes, group):
            x = jnp.concatenate(
                [lines_in[pl.ds(base + g, 2 * A, stride=sublanes), :] for g in range(group)], axis=1
            )
            y = dot3((m2h[...], m2l[...]), split(x))
            parts = []
            for g in range(group):
                yr = y[:A, g * lanes : (g + 1) * lanes]
                yi = y[A:, g * lanes : (g + 1) * lanes]
                parts.append(jnp.concatenate([yr * tr - yi * ti, yr * ti + yi * tr], axis=1))
            u = dot3(split(jnp.concatenate(parts, axis=0)), (m3h[...], m3l[...]))
            ur, ui = u[:, :lanes], u[:, lanes:]
            mag = -(ur * ur + ui * ui)
            cubic = jnp.concatenate([mag * (ur - beta * ui), mag * (ui + beta * ur)], axis=1)
            y = dot3(split(cubic), (n3h[...], n3l[...]))
            parts = []
            for g in range(group):
                yr = y[g * A : (g + 1) * A, :lanes]
                yi = y[g * A : (g + 1) * A, lanes:]
                parts.append(jnp.concatenate([yr * tr + yi * ti, yi * tr - yr * ti], axis=0))
            h, l = split(jnp.concatenate(parts, axis=1))
            pxh[:, base * lanes : (base + group) * lanes] = h
            pxl[:, base * lanes : (base + group) * lanes] = l
        count = part_k * D
        for chunk in range(chunks):
            rows = pl.ds(chunk * 2 * count, 2 * count)
            x = dot3((n2h[rows, :], n2l[rows, :]), (pxh[...], pxl[...]))
            for part in range(2):
                for g in range(sublanes):
                    at = (part * K + chunk * part_k) * D * sublanes + g
                    lines_out[pl.ds(at, count, stride=sublanes), :] = x[
                        part * count : (part + 1) * count, g * lanes : (g + 1) * lanes
                    ]
            start(0, chunk)

    E, E2, Q, F1, F2, F3 = range(6)

    def weight(n, k, at):
        return pair(wts.at[n], k, at)

    def add(a, b):
        return a[0] + b[0], a[1] + b[1]

    first = flat(recv.at[0])
    for chunk in range(chunks):
        finish(0, chunk)

        def take(b):
            at = row_at(b)
            for k in blocks(chunk):
                v = pair(first, k, at)
                put_split(xbh, xbl, k, at, v)
                put(astate, k, at, v)

        loop(R // rb, take)
        launch(1, chunk)

    def hidden(body):
        def block(b):
            for k in range(K):
                body(k, row_at(b))

        loop(R // rb, block)

    def hide_start(k, at):
        v = pair(astate, k, at)
        put(acc, k, at, times(weight(E, k, at), v))
        put(pre, k, at, times(weight(E2, k, at), v))

    def use_first(k, at, n):
        a = add(pair(pre, k, at), times(weight(Q, k, at), n))
        put(nl, k, at, n)
        put(astate, k, at, a)
        put_split(xbh, xbl, k, at, a)

    def hide_first(k, at):
        n = pair(nl, k, at)
        put(acc, k, at, add(pair(acc, k, at), times(weight(F1, k, at), n)))
        qn = times(weight(Q, k, at), n)
        ea = times(weight(E2, k, at), pair(astate, k, at))
        put(astate, k, at, (ea[0] - qn[0], ea[1] - qn[1]))

    def use_second(k, at, n):
        b = add(pair(pre, k, at), times(weight(Q, k, at), n))
        put(nl, k, at, n)
        put_split(xbh, xbl, k, at, b)

    def hide_middle(k, at):
        n = pair(nl, k, at)
        put(acc, k, at, add(pair(acc, k, at), times(weight(F2, k, at), n)))

    def use_third(k, at, n):
        qn = times(weight(Q, k, at), n)
        put(nl, k, at, n)
        a = pair(astate, k, at)
        put_split(xbh, xbl, k, at, (a[0] + 2.0 * qn[0], a[1] + 2.0 * qn[1]))

    def use_last(k, at, n):
        put(send_flat, k, at, add(pair(acc, k, at), times(weight(F3, k, at), n)))

    uses = (use_first, use_second, use_third, use_last)
    hides = (hide_start, hide_first, hide_middle, hide_middle)
    for stage in range(4):
        hidden(hides[stage])
        for chunk in range(chunks):
            finish(1, chunk)
        physics(1)
        for chunk in range(chunks):
            finish(0, chunk)
            land(0, chunk, uses[stage])
            if stage < 3:
                launch(1, chunk)
            else:
                start(1, chunk)

    for chunk in range(chunks):
        finish(1, chunk)

        def leave(d):
            for k in blocks(chunk):
                at = pl.multiple_of(d * span + k * lanes, lanes)
                out_ref[:, :, pl.ds(at, lanes)] = recv[1, :, k, d]

        loop(D, leave)


def solution(mesh):
    axes = ("gx", "gy")
    Z, G = mesh.shape["gx"], mesh.shape["gy"]
    D = Z * G

    def local(spectrum, parameters):
        _, row_shard, columns = spectrum.shape
        assert row_shard == sublanes
        R = row_shard * D
        A = columns // lanes
        K = A // D
        assert K * D * lanes == columns
        counter = np.arange(R)
        m1 = halves(real_form(unit_roots(counter, counter, R)))
        order = (np.arange(D)[None, :] * K + np.arange(K)[:, None]).reshape(-1)
        m2_full = real_form(unit_roots(np.arange(A), order, A))
        chunks = 2 if K % 2 == 0 else 1
        sent = np.arange(2 * A).reshape(2, chunks, A // chunks).swapaxes(0, 1).reshape(-1)
        m2, n2 = halves(m2_full), halves(m2_full.T[sent])
        m3_full = real_form(unit_roots(np.arange(lanes), np.arange(lanes), lanes)).T
        m3, n3 = halves(m3_full), halves(m3_full.T)
        turn = unit_roots(np.arange(A), np.arange(lanes), columns)
        t2 = jnp.asarray(np.stack([turn.real, turn.imag]), jnp.float32)
        vmem = pl.BlockSpec(memory_space=pltpu.VMEM)
        state = pltpu.VMEM((2, K, R, lanes), jnp.float32)
        half = pltpu.VMEM((2 * R, K // chunks * lanes), jnp.bfloat16)
        line = pltpu.VMEM((2 * A, sublanes * lanes), jnp.bfloat16)
        return pl.pallas_call(
            functools.partial(kernel, axes, (Z, G, D, K, R)),
            out_shape=jax.ShapeDtypeStruct(spectrum.shape, jnp.float32),
            in_specs=[pl.BlockSpec(memory_space=pltpu.SMEM)] + [vmem] * 12,
            out_specs=vmem,
            scratch_shapes=[
                pltpu.VMEM((2, K, D, sublanes, lanes), jnp.float32),
                pltpu.VMEM((2, 2, K, D, sublanes, lanes), jnp.float32),
                pltpu.VMEM((6, 2, K, R, lanes), jnp.float32),
                state, state, state, state, state,
                half, half, half, half, line, line,
                pltpu.SemaphoreType.DMA((chunks, D)),
                pltpu.SemaphoreType.DMA((2, chunks, D)),
            ],
            compiler_params=pltpu.CompilerParams(
                collective_id=0, has_side_effects=True, vmem_limit_bytes=60 * 1024 * 1024
            ),
        )(parameters, spectrum, *m1, *m2, *n2, *m3, *n3, t2)

    return jax.shard_map(
        local,
        mesh=mesh,
        in_specs=(P(None, axes, None), P()),
        out_specs=P(None, axes, None),
        check_vma=False,
    )
```

time: 596 us -> 255 us (0.43); the launches traced: 585 us -> 255 us
  Pallas kernels: 0 us -> 253 us
  matrix products: 186 us -> 0 us
  blocking collectives: 178 us -> 0 us
  waiting for transfers between devices: 82.8 us -> 0 us
  local copies, waits for them, and re-layouts: 67.7 us -> 2.26 us
  other arithmetic: 48.9 us -> 0 us
  starting transfers between devices: 18.5 us -> 0 us
    pallas_call x0 -> x1, Pallas kernels: none -> 253 us  [local(): pl.pallas_call(functools.partial(kernel, axes, (Z, G, D, K, R)), out_shap...]
    dot_general x128 -> x0, matrix products: 186 us -> none  [the longest x32 49.4 us: complex_section(): jnp.einsum(formula, sine_part, latter, precision=highest)]
    all_to_all x6 -> x0, blocking collectives: 178 us -> none  [the longest x3 88.9 us: physical_pass(): lax.all_to_all(turned.reshape(2, devices, row_shard, col_shard), ('gx', '...]
    all_to_all x4 -> x0, waiting for transfers between devices: 82.8 us -> none  [the longest x2 34 us: physical_pass(): lax.all_to_all(turned_back.reshape(2, row_shard, devices, col_shard), ('g...]
    sub x14 -> x0, other arithmetic: 42.6 us -> none  [the longest x13 42.2 us: complex_times(): factor[0] * operand[0] - factor[1] * operand[1]]
    another operation x32 -> x0, local copies, waits for them, and re-layouts: 20.3 us -> none  [the longest x8 6.6 us: dft_first(): parts[0].reshape(radix_size, remain, breadth)]
    all_to_all x4 -> x0, starting transfers between devices: 18.5 us -> none  [the longest x2 7.54 us: physical_pass(): lax.all_to_all(turned_back.reshape(2, row_shard, devices, col_shard), ('g...]
    slice x20 -> x0, local copies, waits for them, and re-layouts: 12.6 us -> none  [the longest x12 6 us: physics(): physical = dft_last((received[0, 0], received[1, 0]), 1.0)]
  transfers between devices with their start and end apart: 4 -> 0, of which waited for: 4 -> 0; matrix products, arithmetic and copies ran while one was open for 3% -> 0% of each run, Pallas kernels for 0% -> 0%
where the time goes in v1:
time: 255 us
  Pallas kernels  253 us (99%)
    pallas_call x1, Pallas kernels, local(): pl.pallas_call(functools.partial(kernel, axes, (Z, G, D, K, R)), out_shap...  253 us

profile of v1, /device:TPU:0, one launch (start us, length us, event | category | flops | bytes accessed | tf_op | source)
XLA Modules:
  0.0 255.1 jit_solution(3679876900439477211)
XLA Ops:
  0.0 252.9 %shard_map.127 = f32[2,8,16384]{2,1,0:T(8,128)} custom-call(f32[2]{0:T(128)} %par_ref.1, f32[2,8,16384]{2,1,0:T(8,128)} %spec_ref.1, bf16[512,512]{1,0:T(8,128)(2,1)} %constant.19.m1h, bf16[512,512]{1,0:T(8,128)(2,1)} %constant.22.m1l, bf16[256,256]{1,0:T(8,128)(2,1)} %constant.23.m2h, bf16[256,256]{1,0:T(8,128)(2,1)} %constant.26.m2l, ...), custom_call_target="tpu_custom_call" | custom-call | tf_op jit(solution)/shard_map/pallas_call | solution.py:433
  252.9 2.3 copy.15

commit v2 on v1

--- a/solution.py
+++ b/solution.py
@@ -140,13 +140,16 @@
             device_id_type=mesh_type,
         )
 
+    def blocks(chunk):
+        return [(place, chunk * part_k + place) for place in range(part_k)]
+
     def start(slot, chunk):
         def body(i, carry):
             copy(slot, chunk, i, None).start()
             return carry
 
         lax.fori_loop(1, D, body, 0)
-        for k in range(chunk * part_k, (chunk + 1) * part_k):
+        for _, k in blocks(chunk):
             recv[slot, :, k, me] = send[:, k, me]
 
     def finish(slot, chunk):
@@ -213,10 +216,10 @@
         ref[0, k, pl.ds(at, rb)] = value[0]
         ref[1, k, pl.ds(at, rb)] = value[1]
 
-    def put_split(high, low, k, at, value):
+    def put_split(high, low, place, at, value):
         for part in range(2):
             h, l = split(value[part])
-            k0 = k % part_k * lanes
+            k0 = place * lanes
             high[pl.ds(part * R + at, rb), k0 : k0 + lanes] = h
             low[pl.ds(part * R + at, rb), k0 : k0 + lanes] = l
 
@@ -227,12 +230,8 @@
             for part in range(2)
         )
 
-    def lane_block(value, k):
-        k0 = k % part_k * lanes
-        return value[:, k0 : k0 + lanes]
-
-    def blocks(chunk):
-        return range(chunk * part_k, (chunk + 1) * part_k)
+    def lane_block(value, place):
+        return value[:, place * lanes : (place + 1) * lanes]
 
     def row_at(b):
         return pl.multiple_of(b * rb, rb)
@@ -243,8 +242,8 @@
         def body(b):
             at = row_at(b)
             real, imag = column_dot(xbh, xbl, at)
-            for k in blocks(chunk):
-                turned = times((lane_block(real, k), lane_block(imag, k)), pair(t1, k, at))
+            for place, k in blocks(chunk):
+                turned = times((lane_block(real, place), lane_block(imag, place)), pair(t1, k, at))
                 put(send_flat, k, at, turned)
 
         loop(R // rb, body)
@@ -255,19 +254,19 @@
 
         def turn(b):
             at = row_at(b)
-            for k in blocks(chunk):
+            for place, k in blocks(chunk):
                 x = pair(arrived, k, at)
                 t = pair(t1, k, at)
                 value = (x[0] * t[0] + x[1] * t[1], x[0] * t[1] - x[1] * t[0])
-                put_split(xah, xal, k, at, value)
+                put_split(xah, xal, place, at, value)
 
         loop(R // rb, turn)
 
         def body(b):
             at = row_at(b)
             real, imag = column_dot(xah, xal, at)
-            for k in blocks(chunk):
-                use(k, at, (lane_block(real, k), -lane_block(imag, k)))
+            for place, k in blocks(chunk):
+                use(place, k, at, (lane_block(real, place), -lane_block(imag, place)))
 
         loop(R // rb, body)
 
@@ -326,9 +325,9 @@
 
         def take(b):
             at = row_at(b)
-            for k in blocks(chunk):
+            for place, k in blocks(chunk):
                 v = pair(first, k, at)
-                put_split(xbh, xbl, k, at, v)
+                put_split(xbh, xbl, place, at, v)
                 put(astate, k, at, v)
 
         loop(R // rb, take)
@@ -336,21 +335,20 @@
 
     def hidden(body):
         def block(b):
-            for k in range(K):
-                body(k, row_at(b))
-
-        loop(R // rb, block)
+            body(lax.rem(b, K), row_at(b // K))
+
+        loop(R // rb * K, block)
 
     def hide_start(k, at):
         v = pair(astate, k, at)
         put(acc, k, at, times(weight(E, k, at), v))
         put(pre, k, at, times(weight(E2, k, at), v))
 
-    def use_first(k, at, n):
+    def use_first(place, k, at, n):
         a = add(pair(pre, k, at), times(weight(Q, k, at), n))
         put(nl, k, at, n)
         put(astate, k, at, a)
-        put_split(xbh, xbl, k, at, a)
+        put_split(xbh, xbl, place, at, a)
 
     def hide_first(k, at):
         n = pair(nl, k, at)
@@ -359,22 +357,22 @@
         ea = times(weight(E2, k, at), pair(astate, k, at))
         put(astate, k, at, (ea[0] - qn[0], ea[1] - qn[1]))
 
-    def use_second(k, at, n):
+    def use_second(place, k, at, n):
         b = add(pair(pre, k, at), times(weight(Q, k, at), n))
         put(nl, k, at, n)
-        put_split(xbh, xbl, k, at, b)
+        put_split(xbh, xbl, place, at, b)
 
     def hide_middle(k, at):
         n = pair(nl, k, at)
         put(acc, k, at, add(pair(acc, k, at), times(weight(F2, k, at), n)))
 
-    def use_third(k, at, n):
+    def use_third(place, k, at, n):
         qn = times(weight(Q, k, at), n)
         put(nl, k, at, n)
         a = pair(astate, k, at)
-        put_split(xbh, xbl, k, at, (a[0] + 2.0 * qn[0], a[1] + 2.0 * qn[1]))
-
-    def use_last(k, at, n):
+        put_split(xbh, xbl, place, at, (a[0] + 2.0 * qn[0], a[1] + 2.0 * qn[1]))
+
+    def use_last(place, k, at, n):
         put(send_flat, k, at, add(pair(acc, k, at), times(weight(F3, k, at), n)))
 
     uses = (use_first, use_second, use_third, use_last)
@@ -384,7 +382,8 @@
         for chunk in range(chunks):
             finish(1, chunk)
         physics(1)
-        for chunk in range(chunks):
+
+        def column_side(chunk):
             finish(0, chunk)
             land(0, chunk, uses[stage])
             if stage < 3:
@@ -392,11 +391,13 @@
             else:
                 start(1, chunk)
 
+        loop(chunks, column_side)
+
     for chunk in range(chunks):
         finish(1, chunk)
 
         def leave(d):
-            for k in blocks(chunk):
+            for place, k in blocks(chunk):
                 at = pl.multiple_of(d * span + k * lanes, lanes)
                 out_ref[:, :, pl.ds(at, lanes)] = recv[1, :, k, d]
 

time: 255 us -> 256 us (level)
  no operation moved by 1% of the time
where the time goes in v2:
time: 256 us; the launch traced here: 255 us
  Pallas kernels  253 us (99%)
    pallas_call x1, Pallas kernels, local(): pl.pallas_call(functools.partial(kernel, axes, (Z, G, D, K, R)), out_shap...  253 us

profile of v2, /device:TPU:0, one launch (start us, length us, event | category | flops | bytes accessed | tf_op | source)
XLA Modules:
  0.0 255.3 jit_solution(11659418700180800722)
XLA Ops:
  0.0 253.1 %shard_map.127 = f32[2,8,16384]{2,1,0:T(8,128)} custom-call(f32[2]{0:T(128)} %par_ref.1, f32[2,8,16384]{2,1,0:T(8,128)} %spec_ref.1, bf16[512,512]{1,0:T(8,128)(2,1)} %constant.19.m1h, bf16[512,512]{1,0:T(8,128)(2,1)} %constant.22.m1l, bf16[256,256]{1,0:T(8,128)(2,1)} %constant.23.m2h, bf16[256,256]{1,0:T(8,128)(2,1)} %constant.26.m2l, ...), custom_call_target="tpu_custom_call" | custom-call | tf_op jit(solution)/shard_map/pallas_call | solution.py:434
  253.1 2.3 copy.15
